TPU v7x, 16 devices: a 4x2x1 block of a 4x4x8 slice. The times are simulated.
16 devices in a mesh: rep: 2 (over y, z), dp: 8 (over x, core).
Axes of the slice: x: 4, y: 2, z: 1, core: 2. Of those that a mesh axis runs over, the one named last changes fastest.
The devices are a block of a 4x4x8 slice.
Arguments:
- x: bfloat16 [16, 2048, 1024], P(('rep', 'dp')), parts along dimension 0
- dy: bfloat16 [16, 2048, 1024], P(('rep', 'dp')), parts along dimension 0
- w_gate: bfloat16 [2, 1024, 3200], P(None, 'dp')
- w_up: bfloat16 [2, 1024, 3200], P(None, 'dp')
- w_down: bfloat16 [2, 3200, 1024], P(None, 'dp')
Outputs:
- output 1: bfloat16 [16, 2048, 1024], P(('rep', 'dp')), parts along dimension 0
- output 2: bfloat16 [4, 1024, 3200], P('rep', 'dp'), parts along dimension 0
- output 3: bfloat16 [4, 1024, 3200], P('rep', 'dp'), parts along dimension 0
- output 4: bfloat16 [4, 3200, 1024], P('rep', 'dp'), parts along dimension 0
There are 2 independent parts. A program takes and returns all parts, laid end to end along the dimension named above; an argument that names none is the same for every part.
All inputs are finite; a program needn't handle non-finite values.
Results may differ from a plain program's by a relative error of at most 0.018.
Values are sent between devices in bfloat16 or wider.
A program may use at most 768 MiB of HBM per device.

v0:
```python
import jax
import jax.numpy as jnp
from jax import lax

NAMES = ("w_gate", "w_up", "w_down")


def matmul(a, w):
    return jnp.dot(a, w, preferred_element_type=jnp.float32).astype(jnp.bfloat16)


def normed(h):
    wide = h.astype(jnp.float32)
    scale = lax.rsqrt(jnp.mean(wide**2, -1, keepdims=True) + 1e-6)
    return (wide * scale).astype(jnp.bfloat16)


def layer(h, w):
    a = normed(h)
    gate = jnp.dot(a, w["w_gate"], preferred_element_type=jnp.float32)
    up = jnp.dot(a, w["w_up"], preferred_element_type=jnp.float32)
    return h + matmul((jax.nn.silu(gate) * up).astype(jnp.bfloat16), w["w_down"])


def stack(weights, h):
    for number in range(weights["w_gate"].shape[0]):
        h = layer(h, {name: w[number] for name, w in weights.items()})
    return h


def solution(mesh):
    groups = mesh.shape["rep"]

    def step(x, dy, *weights):
        shape = x.shape
        x, dy = (t.reshape(groups, -1, *t.shape[1:]) for t in (x, dy))

        def of_a_group(x, dy):
            _, back = jax.vjp(stack, dict(zip(NAMES, weights, strict=True)), x)
            by_weights, by_x = back(dy)
            return (by_x, *(by_weights[name] for name in NAMES))

        by_x, *by_weights = jax.vmap(of_a_group)(x, dy)
        return (by_x.reshape(shape), *(t.reshape(-1, *t.shape[2:]) for t in by_weights))

    return step
```

profile of v0, /device:TPU:112, one launch (start us, length us, event | category | flops | bytes accessed | tf_op | source)
XLA Modules:
  0.0 755.1 jit_solution(17519468613207546329)
XLA Ops:
  7.2 0.1 all-gather.30.cloned.1.call-start
  7.3 2.8 fusion.101
  10.1 0.1 all-gather.32.cloned.1.call-start
  10.2 2.7 fusion.100
  12.9 0.1 all-gather.34.cloned.1.call-start
  13.0 1.3 fusion.102
  14.4 0.1 all-gather.36.cloned.1.call-start
  14.5 0.6 all-gather.36.cloned.1.call-update
  15.0 0.1 all-gather.40.cloned.1.call-start
  15.1 0.6 all-gather.40.cloned.1.call-update
  15.7 0.1 all-gather.38.cloned.1.call-start
  15.7 0.6 all-gather.38.cloned.1.call-update
  16.3 0.1 reduce-scatter.27.cloned.1.call-start
  16.4 3.1 fusion.41
  19.5 6.4 copy.1
  25.9 0.6 multiply_add_fusion.1
  26.5 24.3 %all-gather.30.cloned.1.call-done = bf16[1,1024,3200]{2,1,0:T(8,128)(2,1)} async-done(((bf16[1,128,3200]{2,1,0:T(8,128)(2,1)}), bf16[1,1024,3200]{2,1,0:T(8,128)(2,1)}) %all-gather.30.cloned.1.call-update) | async-done | bytes 6553616 | tf_op jit(solution)/vmap(jvp())/squeeze | solution.py:27
  50.8 21.9 %fusion.68 = f32[2048,3200]{1,0:T(8,128)} fusion(bf16[1,1024,3200]{2,1,0:T(8,128)(2,1)} %all-gather.30.cloned.1.call-done, bf16[1,2048,1024]{2,1,0:T(8,128)(2,1)} %param.1, f32[2048]{0:T(1024)S(1)} %get-tuple-element.13), kind=kOutput, calls=%fused_computation.87 | convolution fusion | flops 13428064256 | bytes 36970496 | tf_op jit(solution)/vmap(jvp())/dot_general | solution.py:20
  72.6 18.1 %all-gather.32.cloned.1.call-done = bf16[1,1024,3200]{2,1,0:T(8,128)(2,1)} async-done(((bf16[1,128,3200]{2,1,0:T(8,128)(2,1)}), bf16[1,1024,3200]{2,1,0:T(8,128)(2,1)}) %all-gather.32.cloned.1.call-update) | async-done | bytes 6553616 | tf_op jit(solution)/vmap(jvp())/squeeze | solution.py:27
  90.7 21.9 %fusion.64 = f32[2048,3200]{1,0:T(8,128)} fusion(bf16[1,1024,3200]{2,1,0:T(8,128)(2,1)} %all-gather.32.cloned.1.call-done, bf16[1,2048,1024]{2,1,0:T(8,128)(2,1)} %param.1, f32[2048]{0:T(1024)S(1)} %get-tuple-element.13), kind=kOutput, calls=%fused_computation.83 | convolution fusion | flops 13428064256 | bytes 36970496 | tf_op jit(solution)/vmap(jvp())/dot_general | solution.py:21
  112.6 23.0 %fusion.24 = bf16[2048,3200]{1,0:T(8,128)(2,1)} fusion(f32[2048,3200]{1,0:T(8,128)} %fusion.64, f32[2048,3200]{1,0:T(8,128)} %fusion.68), kind=kLoop, calls=%fused_computation.40 | loop fusion | flops 39321600 | bytes 65536000
  135.6 22.1 %fusion.49 = (f32[2048]{0:T(1024)S(1)}, bf16[1,1,2048,1024]{2,3,1,0:T(8,128)(2,1)}) fusion(bf16[2048,3200]{1,0:T(8,128)(2,1)} %fusion.24, bf16[1,3200,1024]{2,1,0:T(8,128)(2,1)} %all-gather.34.cloned.1.call-done, bf16[1,2048,1024]{1,2,0:T(8,128)(2,1)} %copy.1), kind=kOutput, calls=%fused_computation.68 | convolution fusion | flops 13432256512 | bytes 28057600 | tf_op jit(solution)/vmap(jvp())/dot_general | solution.py:9
  157.7 0.6 copy-done.5
  158.3 11.7 %all-gather.36.cloned.1.call-done = bf16[1,1024,3200]{2,1,0:T(8,128)(2,1)} async-done(((bf16[1,128,3200]{2,1,0:T(8,128)(2,1)}), bf16[1,1024,3200]{2,1,0:T(8,128)(2,1)}) %all-gather.36.cloned.1.call-update) | async-done | bytes 6553616 | tf_op jit(solution)/vmap(jvp())/squeeze | solution.py:27
  169.9 23.3 %fusion.58 = f32[2048,3200]{1,0:T(8,128)} fusion(bf16[1,1024,3200]{2,1,0:T(8,128)(2,1)} %all-gather.36.cloned.1.call-done, bf16[1,1,2048,1024]{2,3,1,0:T(8,128)(2,1)} %get-tuple-element.15, f32[2048]{0:T(1024)S(1)} %bitcast.259), kind=kOutput, calls=%fused_computation.77 | convolution fusion | flops 13428064256 | bytes 36970496 | tf_op jit(solution)/vmap(jvp())/dot_general | solution.py:20
  193.2 16.5 %all-gather.40.cloned.1.call-done = bf16[1,1024,3200]{2,1,0:T(8,128)(2,1)} async-done(((bf16[1,128,3200]{2,1,0:T(8,128)(2,1)}), bf16[1,1024,3200]{2,1,0:T(8,128)(2,1)}) %all-gather.40.cloned.1.call-update) | async-done | bytes 6553616 | tf_op jit(solution)/vmap(jvp())/squeeze | solution.py:27
  209.8 23.0 %fusion.52 = f32[2048,3200]{1,0:T(8,128)} fusion(bf16[1,1024,3200]{2,1,0:T(8,128)(2,1)} %all-gather.40.cloned.1.call-done, bf16[1,1,2048,1024]{2,3,1,0:T(8,128)(2,1)} %get-tuple-element.15, f32[2048]{0:T(1024)S(1)} %bitcast.260), kind=kOutput, calls=%fused_computation.71 | convolution fusion | flops 13428064256 | bytes 36970496 | tf_op jit(solution)/vmap(jvp())/dot_general | solution.py:21
  232.7 27.9 %fusion.32 = f32[1,3200,1024]{2,1,0:T(8,128)} fusion(f32[2048,3200]{1,0:T(8,128)} %fusion.52, f32[2048,3200]{1,0:T(8,128)} %fusion.58, bf16[1,2048,1024]{2,1,0:T(8,128)(2,1)} %param), kind=kOutput, calls=%fused_computation.54 | convolution fusion | flops 13461094400 | bytes 69730304 | tf_op jit(solution)/vmap(transpose(jvp()))/dot_general | solution.py:9
  260.7 0.1 reduce-scatter.29.cloned.1.call-start
  260.8 6.7 copy
  267.5 20.7 %convolution_convert_fusion.1 = bf16[2048,3200]{1,0:T(8,128)(2,1)} fusion(bf16[1,3200,1024]{2,1,0:T(8,128)(2,1)} %all-gather.38.cloned.1.call-done, bf16[1,2048,1024]{2,1,0:T(8,128)(2,1)} %param), kind=kOutput, calls=%fused_computation.35 | convolution fusion | flops 13428326400 | bytes 23855104 | tf_op jit(solution)/vmap(transpose(jvp()))/dot_general | solution.py:9
  288.2 26.9 %fusion.4 = bf16[2048,3200]{1,0:T(8,128)(2,1)} fusion(f32[2048,3200]{1,0:T(8,128)} %fusion.58, f32[2048,3200]{1,0:T(8,128)} %fusion.52, bf16[2048,3200]{1,0:T(8,128)(2,1)} %convolution_convert_fusion.1), kind=kLoop, calls=%fused_computation.10 | loop fusion | flops 78643200 | bytes 78643200
  315.1 22.6 %fusion.22 = bf16[2048,1024]{0,1:T(8,128)(2,1)} fusion(bf16[2048,3200]{1,0:T(8,128)(2,1)} %convolution_convert_fusion.1, f32[2048,3200]{1,0:T(8,128)} %fusion.58, bf16[1,1024,3200]{2,1,0:T(8,128)(2,1)} %all-gather.40.cloned.1.call-done), kind=kOutput, calls=%fused_computation.33 | convolution fusion | flops 13461094400 | bytes 50069504 | tf_op jit(solution)/vmap(transpose(jvp()))/dot_general | solution.py:21
  337.7 20.2 %fusion.51 = (f32[2048]{0:T(1024)S(1)}, bf16[2048,1024]{0,1:T(8,128)(2,1)S(1)}) fusion(bf16[1,1,2048,1024]{2,3,1,0:T(8,128)(2,1)S(1)} %copy-done.3, bf16[2048,1024]{0,1:T(8,128)(2,1)} %fusion.22, bf16[2048,3200]{1,0:T(8,128)(2,1)} %fusion.4, bf16[1,1024,3200]{2,1,0:T(8,128)(2,1)} %all-gather.36.cloned.1.call-done), kind=kOutput, calls=%fused_computation.70 | convolution fusion | flops 13432256512 | bytes 32251904 | tf_op jit(solution)/vmap(transpose(jvp()))/dot_general | solution.py:20
  358.0 3.2 fusion.74
  361.2 2.0 copy-done
  363.2 19.7 %convolution_bitcast_fusion.2 = f32[1,3200,1024]{2,1,0:T(8,128)} fusion(bf16[2048,3200]{1,0:T(8,128)(2,1)} %fusion.24, bf16[1,1,2048,1024]{2,3,1,0:T(8,128)(2,1)S(1)} %fusion.74), kind=kOutput, calls=%fused_computation.59 | convolution fusion | flops 13421772800 | bytes 30408704 | tf_op jit(solution)/vmap(transpose(jvp()))/dot_general | solution.py:9
  383.0 0.1 reduce-scatter.23.cloned.1.call-start
  383.1 26.0 %fusion.35 = f32[1,1024,3200]{2,1,0:T(8,128)} fusion(bf16[2048,3200]{1,0:T(8,128)(2,1)} %convolution_convert_fusion.1, f32[2048,3200]{1,0:T(8,128)} %fusion.58, bf16[1,1,2048,1024]{2,3,1,0:T(8,128)(2,1)} %get-tuple-element.15, f32[2048]{0:T(1024)S(1)} %bitcast.262), kind=kOutput, calls=%fused_computation.55 | convolution fusion | flops 13467385856 | bytes 56631296 | tf_op jit(solution)/vmap(transpose(jvp()))/dot_general | solution.py:21
  409.1 0.1 reduce-scatter.25.cloned.1.call-start
  409.2 21.0 %convolution_convert_fusion = bf16[2048,3200]{1,0:T(8,128)(2,1)} fusion(bf16[1,3200,1024]{2,1,0:T(8,128)(2,1)} %all-gather.34.cloned.1.call-done, bf16[1,1,2048,1024]{2,3,1,0:T(8,128)(2,1)} %copy-done), kind=kOutput, calls=%fused_computation.34 | convolution fusion | flops 13428326400 | bytes 23855104 | tf_op jit(solution)/vmap(transpose(jvp()))/dot_general | solution.py:9
  430.2 26.9 %fusion.7 = bf16[2048,3200]{1,0:T(8,128)(2,1)} fusion(f32[2048,3200]{1,0:T(8,128)} %fusion.68, f32[2048,3200]{1,0:T(8,128)} %fusion.64, bf16[2048,3200]{1,0:T(8,128)(2,1)} %convolution_convert_fusion), kind=kLoop, calls=%fused_computation.13 | loop fusion | flops 78643200 | bytes 78643200
  457.0 21.4 %fusion.18 = bf16[2048,1024]{0,1:T(8,128)(2,1)S(1)} fusion(bf16[2048,3200]{1,0:T(8,128)(2,1)} %convolution_convert_fusion, f32[2048,3200]{1,0:T(8,128)} %fusion.68, bf16[1,1024,3200]{2,1,0:T(8,128)(2,1)} %all-gather.32.cloned.1.call-done), kind=kOutput, calls=%fused_computation.31 | convolution fusion | flops 13461094400 | bytes 50069504 | tf_op jit(solution)/vmap(transpose(jvp()))/dot_general | solution.py:21
  478.4 20.3 %fusion.47 = (f32[2048]{0:T(1024)S(1)}, bf16[2048,1024]{0,1:T(8,128)(2,1)}) fusion(bf16[1,2048,1024]{1,2,0:T(8,128)(2,1)S(1)} %copy-done.1, bf16[2048,1024]{0,1:T(8,128)(2,1)S(1)} %fusion.18, bf16[2048,3200]{1,0:T(8,128)(2,1)} %fusion.7, bf16[1,1024,3200]{2,1,0:T(8,128)(2,1)} %all-gather.30.cloned.1.call-done), kind=kOutput, calls=%fused_computation.66 | convolution fusion | flops 13432256512 | bytes 32251904 | tf_op jit(solution)/vmap(transpose(jvp()))/dot_general | solution.py:20
  498.8 24.6 %fusion.38 = f32[1,1024,3200]{2,1,0:T(8,128)} fusion(bf16[2048,3200]{1,0:T(8,128)(2,1)} %convolution_convert_fusion, f32[2048,3200]{1,0:T(8,128)} %fusion.68, bf16[1,2048,1024]{1,2,0:T(8,128)(2,1)S(1)} %copy-done.1, f32[2048]{0:T(1024)S(1)} %bitcast.264), kind=kOutput, calls=%fused_computation.56 | convolution fusion | flops 13467385856 | bytes 56631296 | tf_op jit(solution)/vmap(transpose(jvp()))/dot_general | solution.py:21
  523.5 0.1 reduce-scatter.19.cloned.1.call-start
  523.6 0.6 copy-done.9
  524.1 22.5 %convolution_bitcast_fusion.1 = f32[1,1024,3200]{2,1,0:T(8,128)} fusion(bf16[2048,3200]{1,0:T(8,128)(2,1)} %fusion.4, bf16[1,1,2048,1024]{2,3,1,0:T(8,128)(2,1)} %get-tuple-element.15, f32[2048]{0:T(1024)S(1)} %bitcast.263), kind=kOutput, calls=%fused_computation.58 | convolution fusion | flops 13428064256 | bytes 30416896 | tf_op jit(solution)/vmap(transpose(jvp()))/dot_general | solution.py:20
  546.7 0.1 reduce-scatter.21.cloned.1.call-start
  546.8 22.0 %convolution_bitcast_fusion = f32[1,1024,3200]{2,1,0:T(8,128)} fusion(bf16[2048,3200]{1,0:T(8,128)(2,1)} %fusion.7, bf16[1,2048,1024]{1,2,0:T(8,128)(2,1)} %copy.1, f32[2048]{0:T(1024)S(1)} %bitcast.265), kind=kOutput, calls=%fused_computation.57 | convolution fusion | flops 13428064256 | bytes 30416896 | tf_op jit(solution)/vmap(transpose(jvp()))/dot_general | solution.py:20
  568.8 7.7 %fusion.73 = bf16[1,2048,1024]{1,2,0:T(8,128)(2,1)} fusion(bf16[1,1,2048,1024]{2,3,1,0:T(8,128)(2,1)} %copy-done, bf16[2048,1024]{0,1:T(8,128)(2,1)} %get-tuple-element.19, bf16[1,2048,1024]{1,2,0:T(8,128)(2,1)} %copy.1, f32[2048]{0:T(1024)S(1)} %bitcast.267, f32[2048]{0:T(1024)S(1)} %bitcast.266), kind=kLoop, calls=%fused_computation.92 | loop fusion | flops 14680064 | bytes 16793600 | tf_op jit(solution)/reshape | solution.py:44
  576.5 6.4 copy.2
  582.9 1.5 convert_bitcast_fusion.1
  584.5 1.5 convert_bitcast_fusion
  586.1 1.3 add_bitcast_fusion
  587.3 1.5 convert_bitcast_fusion.3
  588.9 10.9 %reduce-scatter.25.cloned.1.call-done = f32[1,128,3200]{2,1,0:T(8,128)} async-done(((f32[1,1024,3200]{2,1,0:T(8,128)}), f32[1,128,3200]{2,1,0:T(8,128)}) %reduce-scatter.25.cloned.1.call-update) | async-done | bytes 1638416
  599.7 1.5 convert_bitcast_fusion.2
  601.3 1.3 add_bitcast_fusion.1
  602.6 70.0 %reduce-scatter.19.cloned.1.call-done = f32[1,128,3200]{2,1,0:T(8,128)} async-done(((f32[1,1024,3200]{2,1,0:T(8,128)}), f32[1,128,3200]{2,1,0:T(8,128)}) %reduce-scatter.19.cloned.1.call-update) | async-done | bytes 1638416
  672.6 1.5 convert_bitcast_fusion.5
  674.1 71.2 %reduce-scatter.21.cloned.1.call-done = f32[1,128,3200]{2,1,0:T(8,128)} async-done(((f32[1,1024,3200]{2,1,0:T(8,128)}), f32[1,128,3200]{2,1,0:T(8,128)}) %reduce-scatter.21.cloned.1.call-update) | async-done | bytes 1638416
  745.3 1.5 convert_bitcast_fusion.4
  746.8 1.3 add_bitcast_fusion.2
  (37 shorter events, 0.6 us)
Async XLA Ops:
  7.2 5.8 copy-start.4
  7.2 43.6 %all-gather.30.cloned.1.call-start = ((), (), s32[]{:S(2)}) async-start(), calls=%async_computation.6 | async-start | bytes 7372800 | tf_op jit(solution)/vmap(jvp())/squeeze | solution.py:27
  10.1 80.6 %all-gather.32.cloned.1.call-start = ((), (), s32[]{:S(2)}) async-start(), calls=%async_computation.7 | async-start | bytes 7372800 | tf_op jit(solution)/vmap(jvp())/squeeze | solution.py:27
  12.9 122.6 %all-gather.34.cloned.1.call-start = ((), (), s32[]{:S(2)}) async-start(), calls=%async_computation.8 | async-start | bytes 7372800 | tf_op jit(solution)/vmap(jvp())/squeeze | solution.py:27
  14.4 155.6 %all-gather.36.cloned.1.call-start = ((), (), s32[]{:S(2)}) async-start(), calls=%async_computation.9 | async-start | bytes 7372800 | tf_op jit(solution)/vmap(jvp())/squeeze | solution.py:27
  15.0 194.7 %all-gather.40.cloned.1.call-start = ((), (), s32[]{:S(2)}) async-start(), calls=%async_computation.11 | async-start | bytes 7372800 | tf_op jit(solution)/vmap(jvp())/squeeze | solution.py:27
  15.7 251.8 %all-gather.38.cloned.1.call-start = ((), (), s32[]{:S(2)}) async-start(), calls=%async_computation.10 | async-start | bytes 7372800 | tf_op jit(solution)/vmap(jvp())/squeeze | solution.py:27
  16.3 566.6 %reduce-scatter.27.cloned.1.call-start = ((), (), s32[]{:S(2)}) async-start(), calls=%async_computation.16 | async-start | bytes 14745600
  157.6 0.6 copy-start.5
  158.3 51.5 %copy-start.7 = (f32[1,1,2048]{2,1,0:T(1,128)}, f32[1,1,2048]{2,1,0:T(1,128)S(1)}, u32[]{:S(2)}) copy-start(f32[1,1,2048]{2,1,0:T(1,128)S(1)} %rsqrt.23) | copy-start | bytes 24580
  260.7 323.8 %reduce-scatter.29.cloned.1.call-start = ((), (), s32[]{:S(2)}) async-start(), calls=%async_computation.17 | async-start | bytes 14745600
  315.1 22.6 %copy-start.3 = (bf16[1,1,2048,1024]{2,3,1,0:T(8,128)(2,1)S(1)}, bf16[1,1,2048,1024]{2,3,1,0:T(8,128)(2,1)}, u32[]{:S(2)}) copy-start(bf16[1,1,2048,1024]{2,3,1,0:T(8,128)(2,1)} %get-tuple-element.15) | copy-start | bytes 12582916
  337.7 20.2 %copy-start.6 = (f32[2048]{0:T(1024)S(1)}, f32[2048]{0:T(1024)}, u32[]{:S(2)}) copy-start(f32[2048]{0:T(1024)} %copy-done.5) | copy-start | bytes 24580
  337.7 20.3 %copy-start.2 = (bf16[1,2048,1024]{1,2,0:T(8,128)(2,1)S(1)}, bf16[1,2048,1024]{1,2,0:T(8,128)(2,1)}, u32[]{:S(2)}) copy-start(bf16[1,2048,1024]{1,2,0:T(8,128)(2,1)} %copy) | copy-start | bytes 12582916
  337.7 20.3 %copy-start.8 = (f32[1,1,2048]{2,1,0:T(1,128)S(1)}, f32[1,1,2048]{2,1,0:T(1,128)}, u32[]{:S(2)}) copy-start(f32[1,1,2048]{2,1,0:T(1,128)} %copy-done.7) | copy-start | bytes 24580
  361.2 2.0 copy-start
  383.0 204.3 %reduce-scatter.23.cloned.1.call-start = ((), (), s32[]{:S(2)}) async-start(), calls=%async_computation.14 | async-start | bytes 14745600
  409.1 190.6 %reduce-scatter.25.cloned.1.call-start = ((), (), s32[]{:S(2)}) async-start(), calls=%async_computation.15 | async-start | bytes 14745600
  457.0 21.4 %copy-start.1 = (bf16[1,2048,1024]{1,2,0:T(8,128)(2,1)S(1)}, bf16[1,2048,1024]{1,2,0:T(8,128)(2,1)}, u32[]{:S(2)}) copy-start(bf16[1,2048,1024]{1,2,0:T(8,128)(2,1)} %copy.1) | copy-start | bytes 12582916
  478.4 20.3 %copy-start.10 = (f32[2048]{0:T(1024)S(1)}, f32[2048]{0:T(1024)}, u32[]{:S(2)}) copy-start(f32[2048]{0:T(1024)} %get-tuple-element.12) | copy-start | bytes 24580
  523.4 0.7 copy-start.9
  523.5 149.1 %reduce-scatter.19.cloned.1.call-start = ((), (), s32[]{:S(2)}) async-start(), calls=%async_computation.12 | async-start | bytes 14745600
  546.7 198.6 %reduce-scatter.21.cloned.1.call-start = ((), (), s32[]{:S(2)}) async-start(), calls=%async_computation.13 | async-start | bytes 14745600
Sparse Core Ops, SparseCore 0:
  10.2 40.4 all-gather.29
  52.9 37.7 all-gather.31
  92.3 37.7 all-gather.33
  132.1 37.7 all-gather.35
  171.9 37.7 all-gather.39
  211.2 37.7 all-gather.37
  260.8 71.0 reduce-scatter.26
  383.1 71.0 reduce-scatter.28
  456.5 70.5 reduce-scatter.22
  529.2 70.5 reduce-scatter.24
  602.0 70.5 reduce-scatter.18
  674.8 70.4 reduce-scatter.20
where the time goes:
time: 763 us; the launch traced here: 755 us
  matrix products  381 us (50%)
  waiting for transfers between devices  225 us (29%)
  other arithmetic  104 us (14%)
  local copies, waits for them, and re-layouts  29.6 us (4%)
  between operations  14.6 us (2%)
    unnamed x18, waiting for transfers between devices  154 us
    dot_general x6, matrix products, layer(): up = jnp.dot(a, w['w_up'], preferred_element_type=jnp.float32)  139 us
    dot_general x6, matrix products, layer(): gate = jnp.dot(a, w['w_gate'], preferred_element_type=jnp.float32)  130 us
    dot_general x5, matrix products, matmul(): jnp.dot(a, w, preferred_element_type=jnp.float32).astype(jnp.bfloat16)  111 us
    unnamed x3, other arithmetic  76.7 us
    squeeze x6, waiting for transfers between devices, stack(): h = layer(h, {name: w[number] for name, w in weights.items()})  70.6 us
    unnamed x25, local copies, waits for them, and re-layouts  22.8 us
  transfers between devices with their start and end apart: 12, of which 7 were waited for; matrix products, arithmetic and copies ran while one was open for 67% of the time, Pallas kernels for 0%

commit v1 on v0

v1 whole, which is shorter than its diff:
```python
import functools

import jax
import jax.numpy as jnp
from jax import lax
from jax.experimental import pallas as pl
from jax.experimental.pallas import tpu as pltpu
from jax.sharding import PartitionSpec as P

F32 = jnp.float32
BF = jnp.bfloat16
VMEM_LIMIT = 60 * 1024 * 1024
ANY = pl.BlockSpec(memory_space=pl.ANY)
EPS = 1e-6


def dot(a, b, ca=1, cb=0):
    return lax.dot_general(a, b, (((ca,), (cb,)), ((), ())), preferred_element_type=F32)


def rounded(v):
    return v.astype(BF).astype(F32)


def whole(shape):
    return pl.BlockSpec(shape, lambda *_: (0,) * len(shape), pipeline_mode=pl.Buffered(1))


def params(dims):
    return pltpu.CompilerParams(dimension_semantics=("arbitrary",) * dims, vmem_limit_bytes=VMEM_LIMIT)


def cost(flops, nbytes):
    return pl.CostEstimate(flops=int(flops), bytes_accessed=int(nbytes), transcendentals=0)


def normed(h):
    wide = h.astype(F32)
    return (wide * lax.rsqrt(jnp.mean(wide * wide, -1, keepdims=True) + EPS)).astype(BF)


KINDS = 11


def forward_kernel(n, *refs):
    x_ref, *stacked = refs[:4]
    shards = [w.at[number] for number in range(2) for w in stacked]
    gathered = refs[4:10]
    a0_ref, act_ref, h1_ref, a1_ref = refs[10:14]
    own = refs[14:20]
    x_v, a_v, act_v, wd_v, w_buf, send, recv, load, store, w_sem, act_sem, row_sem = refs[20:]
    T, D = x_ref.shape
    FF = shards[0].shape[1]
    r, i = lax.axis_index("rep"), lax.axis_index("dp")
    nx = n // 2
    x, c = lax.div(i, 2), lax.rem(i, 2)
    q = lax.rem(r, 2)
    s = 1 - 2 * q
    h = 1 - q
    xa = lax.rem(x + s + nx, nx)
    xb = lax.rem(x - s + nx, nx)
    x2 = lax.rem(x + 2, nx)
    to_a, to_b, to_pair, to_core = (r, 2 * xa + c), (r, 2 * xb + c), (r + s, i), (r, 2 * x + 1 - c)

    barrier = pltpu.get_barrier_semaphore()
    for who in (to_a, to_b, to_pair, to_core):
        pl.semaphore_signal(barrier, inc=1, device_id=who, device_id_type=pl.DeviceIdType.MESH)

    def part(ref, base, half):
        rows = shards[0].shape[0] if ref.shape[1] == FF else shards[2].shape[0]
        if ref.shape[1] == FF:
            if half is None:
                return ref.at[pl.ds(pl.multiple_of(base * rows, rows), rows), :]
            return ref.at[pl.ds(pl.multiple_of(base * rows + half * (rows // 2), rows // 2), rows // 2), :]
        at = pl.ds(pl.multiple_of(base * rows, 16), rows)
        if half is None:
            return ref.at[at, :]
        return ref.at[at, pl.ds(pl.multiple_of(half * (D // 2), D // 2), D // 2)]

    def copy(p, kind, arriving=False):
        w = gathered[p]
        src = None
        if kind == 0:
            where, half, there, lands, lhalf, lcore = x, None, to_a, xb, None, c
        elif kind == 1:
            where, half, there, lands, lhalf, lcore = x, h, to_b, xa, h, c
        elif kind == 2:
            where, half, there, lands, lhalf, lcore = xa, h, to_b, x2, h, c
        elif kind == 3:
            where, half, there, lands, lhalf, lcore = xb, h, to_pair, xa, 1 - h, c
        elif kind == 4:
            where, half, there, lands, lhalf, lcore = x2, h, to_pair, x2, 1 - h, c
        else:
            where, half = ((x, None), (xb, None), (xa, h), (x2, h), (xa, 1 - h), (x2, 1 - h))[kind - 5]
            there, lands, lhalf, lcore = to_core, where, half, 1 - c
        dst = part(w, 2 * where + c, half)
        if kind in (0, 1, 5):
            src = part(own[p], 0, half)
        else:
            src = dst
        if arriving:
            src = dst = part(w, 2 * lands + lcore, lhalf)
        return pltpu.make_async_remote_copy(src_ref=src, dst_ref=dst, send_sem=send.at[p, kind], recv_sem=recv.at[p, kind],
                                            device_id=there, device_id_type=pl.DeviceIdType.MESH)

    def go(p, *kinds):
        for k in kinds:
            copy(p, k).start()

    def got(p, *kinds):
        for k in kinds:
            copy(p, k, True).wait_recv()

    def loads(p):
        return pltpu.make_async_copy(shards[p], own[p], load.at[p])

    def stores(p):
        return pltpu.make_async_copy(own[p], part(gathered[p], i, None), store.at[p])

    for p in range(6):
        loads(p).start()

    def start(p):
        loads(p).wait()
        go(p, 1, 0, 5)
        stores(p).start()

    def mid(p):
        got(p, 1)
        go(p, 2)
        got(p, 0)
        go(p, 3, 6, 7)

    def late(p):
        got(p, 2)
        go(p, 4, 8)
        got(p, 3)
        go(p, 9)

    def last(p):
        got(p, 4)
        go(p, 10)

    def done(p):
        got(p, 5, 6, 7, 8, 9, 10)
        stores(p).wait()

    x_load = pltpu.make_async_copy(x_ref, x_v, row_sem.at[0])
    x_load.start()
    pl.semaphore_wait(barrier, 4)
    start(0)
    start(1)

    mt, ft = 256, 256
    full = FF // ft
    rest = FF - full * ft
    x_load.wait()

    def rows_at(m):
        return pl.ds(pl.multiple_of(m * mt, mt), mt)

    @pl.loop(0, T // mt)
    def _(m):
        a_v[rows_at(m), :] = normed(x_v[rows_at(m), :])

    a_out = pltpu.make_async_copy(a_v, a0_ref, row_sem.at[0])
    a_out.start()

    def columns(t, width):
        return pl.ds(pl.multiple_of(t * ft, ft), width)

    def w_copies(t, slot, width):
        return [pltpu.make_async_copy(gathered[k].at[:, columns(t, width)], w_buf.at[k, slot, :, pl.ds(0, width)], w_sem.at[k, slot])
                for k in range(2)]

    def act_out(t, width):
        return pltpu.make_async_copy(act_v.at[:, columns(t, width)], act_ref.at[:, columns(t, width)], act_sem.at[t])

    def act_tile(t, slot, width):
        for cp in w_copies(t, slot, width):
            cp.wait()

        @pl.when(t + 1 < full)
        def _():
            for cp in w_copies(t + 1, 1 - slot, ft):
                cp.start()

        if rest and width == ft:
            @pl.when(t + 1 == full)
            def _():
                for cp in w_copies(t + 1, 1 - slot, rest):
                    cp.start()

        wg_t, wu_t = w_buf[0, slot, :, :width], w_buf[1, slot, :, :width]
        for m in range(T // mt):
            rows = pl.ds(m * mt, mt)
            a = a_v[rows, :]
            g, u = dot(a, wg_t), dot(a, wu_t)
            act_v[rows, columns(t, width)] = (g * jax.nn.sigmoid(g) * u).astype(BF)
        act_out(t, width).start()

    def gate_up(first, last):
        @pl.loop(first, last)
        def _(t):
            act_tile(t, lax.rem(t, 2), ft)

    def down(first, last):
        @pl.loop(first, last)
        def _(m):
            y = dot(act_v[rows_at(m), :], wd_v[...])
            hh = (x_v[rows_at(m), :].astype(F32) + rounded(y)).astype(BF)
            x_v[rows_at(m), :] = hh
            a_v[rows_at(m), :] = normed(hh)

    mid(0)
    start(2)
    late(0)
    mid(1)
    start(3)
    last(0)
    late(1)
    mid(2)
    start(4)
    last(1)
    done(0)
    done(1)
    for cp in w_copies(0, 0, ft):
        cp.start()
    gate_up(0, 3)
    late(2)
    gate_up(3, 7)
    last(2)
    gate_up(7, 9)
    mid(3)
    start(5)
    gate_up(9, full)
    done(2)
    wd_load = pltpu.make_async_copy(gathered[2], wd_v, row_sem.at[1])
    wd_load.start()
    if rest:
        act_tile(full, full % 2, rest)
    late(3)
    a_out.wait()
    wd_load.wait()
    down(0, 2)
    last(3)
    down(2, 4)
    mid(4)
    down(4, T // mt)
    h_out = pltpu.make_async_copy(x_v, h1_ref, row_sem.at[0])
    h_out.start()
    a1_out = pltpu.make_async_copy(a_v, a1_ref, row_sem.at[1])
    a1_out.start()
    late(4)
    mid(5)
    last(4)
    late(5)
    last(5)
    done(3)
    done(4)
    done(5)
    for t in range(full + (rest > 0)):
        act_out(t, ft if t < full else rest).wait()
    h_out.wait()
    a1_out.wait()
    for p in range(6):
        for k in range(KINDS):
            copy(p, k).wait_send()


def forward(n, x, stacked):
    T, D = x.shape
    shards = [jax.ShapeDtypeStruct(w.shape[1:], BF) for _ in range(2) for w in stacked]
    FF = shards[0].shape[1]
    fulls = [jax.ShapeDtypeStruct((w.shape[0] * n, w.shape[1]), BF) for w in shards]
    wide = jax.ShapeDtypeStruct((T, D), BF)
    return pl.pallas_call(
        functools.partial(forward_kernel, n),
        name="gather_forward",
        out_shape=[*fulls, wide, jax.ShapeDtypeStruct((T, FF), BF), wide, wide],
        in_specs=[ANY] * 4,
        out_specs=[ANY] * 10,
        scratch_shapes=[
            *[pltpu.VMEM(w.shape, BF) for w in shards],
            pltpu.VMEM((T, D), BF),
            pltpu.VMEM((T, D), BF),
            pltpu.VMEM((T, FF), BF),
            pltpu.VMEM((FF, D), BF),
            pltpu.VMEM((2, 2, D, 256), BF),
            pltpu.SemaphoreType.DMA((6, KINDS)),
            pltpu.SemaphoreType.DMA((6, KINDS)),
            pltpu.SemaphoreType.DMA((6,)),
            pltpu.SemaphoreType.DMA((6,)),
            pltpu.SemaphoreType.DMA((2, 2)),
            pltpu.SemaphoreType.DMA((pl.cdiv(FF, 256),)),
            pltpu.SemaphoreType.DMA((2,)),
        ],
        compiler_params=pltpu.CompilerParams(collective_id=0, has_side_effects=True, vmem_limit_bytes=VMEM_LIMIT),
        cost_estimate=cost(6 * T * D * FF, 2e8),
    )(x, *stacked)


def inner_backward(a, dy, wg, wu, wd, keep_act):
    T, D = a.shape
    FF = wg.shape[1]
    ft, sub = 256, 256

    def body(a_ref, dy_ref, wg_ref, wu_ref, wd_ref, *outs):
        dg_ref, du_ref = outs[-2:]
        for m in range(T // sub):
            rows = pl.ds(m * sub, sub)
            av = a_ref[rows, :]
            g, u = dot(av, wg_ref[...]), dot(av, wu_ref[...])
            d = rounded(dot(dy_ref[rows, :], wd_ref[...], 1, 1))
            sg = jax.nn.sigmoid(g)
            sl = g * sg
            if keep_act:
                outs[0][rows, :] = (sl * u).astype(BF)
            du_ref[rows, :] = (d * sl).astype(BF)
            dg_ref[rows, :] = (d * u * (sg + sl * (1.0 - sg))).astype(BF)

    col = pl.BlockSpec((D, ft), lambda j: (0, j))
    out = pl.BlockSpec((T, ft), lambda j: (0, j))
    count = 3 if keep_act else 2
    return pl.pallas_call(
        body, name="inner_backward", grid=(pl.cdiv(FF, ft),),
        in_specs=[whole((T, D)), whole((T, D)), col, col, pl.BlockSpec((ft, D), lambda j: (j, 0))],
        out_specs=[out] * count, out_shape=[jax.ShapeDtypeStruct((T, FF), BF)] * count,
        compiler_params=params(1), cost_estimate=cost(6 * T * D * FF, 6e7),
    )(a, dy, wg, wu, wd)


def down_grad(act, dy):
    T, FF = act.shape
    D = dy.shape[1]
    ft = 640

    def body(a_ref, b_ref, o_ref):
        o_ref[...] = dot(a_ref[...], b_ref[...], 0, 0).astype(BF)

    return pl.pallas_call(
        body, name="down_grad", grid=(FF // ft,),
        in_specs=[pl.BlockSpec((T, ft), lambda j: (0, j)), whole((T, D))],
        out_specs=pl.BlockSpec((ft, D), lambda j: (j, 0)), out_shape=jax.ShapeDtypeStruct((FF, D), BF),
        compiler_params=params(1), cost_estimate=cost(2 * T * D * FF, 3e7),
    )(act, dy)


def up_grad(a, dup):
    T, D = a.shape
    FF = dup.shape[1]
    ft = 512

    def body(a_ref, b_ref, o_ref):
        o_ref[...] = dot(a_ref[...], b_ref[...], 0, 0).astype(BF)

    return pl.pallas_call(
        body, name="up_grad", grid=(pl.cdiv(FF, ft),),
        in_specs=[whole((T, D)), pl.BlockSpec((T, ft), lambda j: (0, j))],
        out_specs=pl.BlockSpec((D, ft), lambda j: (0, j)), out_shape=jax.ShapeDtypeStruct((D, FF), BF),
        compiler_params=params(1), cost_estimate=cost(2 * T * D * FF, 3e7),
    )(a, dup)


def input_grad(dgate, dup, wg, wu, h, dh):
    T, FF = dgate.shape
    D = wg.shape[0]
    mt = 256

    def body(g_ref, u_ref, wg_ref, wu_ref, h_ref, dh_ref, o_ref):
        p = rounded(dot(g_ref[...], wg_ref[...], 1, 1))
        q = rounded(dot(u_ref[...], wu_ref[...], 1, 1))
        d = rounded(p + q)
        w = h_ref[...].astype(F32)
        sc = lax.rsqrt(jnp.mean(w * w, -1, keepdims=True) + EPS)
        ds = jnp.sum(d * w, -1, keepdims=True)
        dw = d * sc - w * (ds * sc * sc * sc * (1.0 / D))
        o_ref[...] = (dh_ref[...].astype(F32) + rounded(dw)).astype(BF)

    tf, td = pl.BlockSpec((mt, FF), lambda m: (m, 0)), pl.BlockSpec((mt, D), lambda m: (m, 0))
    return pl.pallas_call(
        body, name="input_grad", grid=(T // mt,), in_specs=[tf, tf, whole((D, FF)), whole((D, FF)), td, td], out_specs=td,
        out_shape=jax.ShapeDtypeStruct((T, D), BF), compiler_params=params(1), cost_estimate=cost(4 * T * D * FF, 5e7),
    )(dgate, dup, wg, wu, h, dh)


def after(value, *others):
    return lax.optimization_barrier((value, *others))[0]


def solution(mesh):
    n = mesh.shape["dp"]

    def step(x, dy, wg, wu, wd):
        x, dy = x[0], dy[0]
        *full, a0, act0, h1, a1 = forward(n, x, (wg, wu, wd))

        def scattered(t):
            return lax.psum_scatter(t, "dp", scatter_dimension=0, tiled=True)

        act1, dg1, du1 = inner_backward(a1, dy, *full[3:], True)
        dwd1 = down_grad(act1, dy)
        sd1 = scattered(dwd1)
        dwg1 = up_grad(a1, after(dg1, dwd1))
        sg1 = scattered(dwg1)
        dwu1 = up_grad(a1, after(du1, dwg1))
        su1 = scattered(dwu1)
        dh1 = input_grad(after(dg1, dwu1, sd1), du1, full[3], full[4], h1, dy)
        dwd0 = down_grad(act0, after(dh1, sg1))
        sd0 = scattered(dwd0)
        dg0, du0 = inner_backward(a0, after(dh1, dwd0), *full[:3], False)
        dwg0 = up_grad(a0, after(dg0, su1))
        sg0 = scattered(dwg0)
        dwu0 = up_grad(a0, after(du0, dwg0))
        su0 = scattered(dwu0)
        dx = input_grad(after(dg0, dwu0), du0, full[0], full[1], x, dh1)
        return dx[None], jnp.stack([sg0, sg1]), jnp.stack([su0, su1]), jnp.stack([sd0, sd1])

    w = P(None, "dp", None)
    return jax.shard_map(
        step, mesh=mesh,
        in_specs=(P(("rep", "dp")), P(("rep", "dp")), w, w, w),
        out_specs=(P(("rep", "dp")), P("rep", "dp"), P("rep", "dp"), P("rep", "dp")),
        check_vma=False,
    )
```

time: 763 us -> 508 us (0.67)
  Pallas kernels: 0 us -> 459 us
  matrix products: 381 us -> 0 us
  waiting for transfers between devices: 225 us -> 18.4 us
  other arithmetic: 104 us -> 7.52 us
  local copies, waits for them, and re-layouts: 29.6 us -> 0.01 us
    pallas_call x0 -> x11, Pallas kernels: none -> 459 us  [the longest x1 152 us: forward(): pl.pallas_call(functools.partial(forward_kernel, n), name='gather_forward...]
    dot_general x17 -> x0, matrix products: 381 us -> none  [the longest x6 139 us: layer(): up = jnp.dot(a, w['w_up'], preferred_element_type=jnp.float32)]
    unnamed x18 -> x6, waiting for transfers between devices: 154 us -> 0.32 us
    unnamed x3 -> x0, other arithmetic: 76.7 us -> none
    squeeze x6 -> x0, waiting for transfers between devices: 70.6 us -> none  [stack(): h = layer(h, {name: w[number] for name, w in weights.items()})]
    unnamed x25 -> x6, local copies, waits for them, and re-layouts: 22.8 us -> 0.01 us
    reduce_scatter x0 -> x6, waiting for transfers between devices: none -> 18.1 us  [scattered(): return lax.psum_scatter(t, 'dp', scatter_dimension=0, tiled=True)]
    reshape x4 -> x0, other arithmetic: 11.6 us -> none  [the longest x1 7.68 us: step(): by_x.reshape(shape)]
  transfers between devices with their start and end apart: 12 -> 6, of which waited for: 7 -> 3; matrix products, arithmetic and copies ran while one was open for 67% -> 1% of each run, Pallas kernels for 0% -> 47%
where the time goes in v1:
time: 508 us; the launch traced here: 499 us
  Pallas kernels  459 us (90%)
  waiting for transfers between devices  18.4 us (4%)
  between operations  14.4 us (3%)
  other arithmetic  7.52 us (1%)
    pallas_call x1, Pallas kernels, forward(): pl.pallas_call(functools.partial(forward_kernel, n), name='gather_forward...  152 us
    pallas_call x2, Pallas kernels, inner_backward(): pl.pallas_call(body, name='inner_backward', grid=(pl.cdiv(FF, ft),), in_s...  105 us
    pallas_call x2, Pallas kernels, input_grad(): pl.pallas_call(body, name='input_grad', grid=(T // mt,), in_specs=[tf, tf...  82.5 us
    pallas_call x4, Pallas kernels, up_grad(): pl.pallas_call(body, name='up_grad', grid=(pl.cdiv(FF, ft),), in_specs=[w...  81.6 us
    pallas_call x2, Pallas kernels, down_grad(): pl.pallas_call(body, name='down_grad', grid=(FF // ft,), in_specs=[pl.Blo...  37.2 us
    reduce_scatter x6, waiting for transfers between devices, scattered(): return lax.psum_scatter(t, 'dp', scatter_dimension=0, tiled=True)  18.1 us
  transfers between devices with their start and end apart: 6, of which 3 were waited for; matrix products, arithmetic and copies ran while one was open for 1% of the time, Pallas kernels for 47%

profile of v1, /device:TPU:112, one launch (start us, length us, event | category | flops | bytes accessed | tf_op | source)
XLA Modules:
  0.0 499.4 jit_solution(14872367483632259597)
XLA Ops:
  7.2 0.1 reduce-scatter.7.cloned.1.call-start
  7.2 151.9 %gather_forward.1 = (bf16[1024,3200]{1,0:T(8,128)(2,1)}, bf16[1024,3200]{1,0:T(8,128)(2,1)}, bf16[3200,1024]{1,0:T(8,128)(2,1)}, bf16[1024,3200]{1,0:T(8,128)(2,...) custom-call(bf16[2048,1024]{1,0:T(8,128)(2,1)} %bitcast.18, ...), custom_call_target="tpu_custom_call" | custom-call | flops 40265318400 | bytes 200000000 | tf_op jit(solution)/shard_map/gather_forward/pallas_call | solution.py:277
  159.1 52.8 %inner_backward.2 = (bf16[2048,3200]{1,0:T(8,128)(2,1)}, bf16[2048,3200]{1,0:T(8,128)(2,1)}, bf16[2048,3200]{1,0:T(8,128)(2,1)}) custom-call(bf16[2048,1024]{1,0:T(8,128)(2,1)} %get-tuple-element.28.a_ref, bf16[2048,1024]{1,0:T(8,128)(2,1)} %bitcast.15, bf16[1024,3200]{1,0:T(8,128)(2,1)} %get-tuple-element.29.wg_ref, ...), custom_call_target="tpu_custom_call" | custom-call | flops 40265318400 | bytes 60000000 | tf_op jit(solution)/shard_map/inner_backward/pallas_call | solution.py:325
  211.9 18.6 %down_grad.2 = bf16[3200,1024]{1,0:T(8,128)(2,1)} custom-call(bf16[2048,3200]{1,0:T(8,128)(2,1)} %get-tuple-element.34.a_ref, bf16[2048,1024]{1,0:T(8,128)(2,1)} %bitcast.16), custom_call_target="tpu_custom_call" | custom-call | flops 13421772800 | bytes 30000000 | tf_op jit(solution)/shard_map/down_grad/pallas_call | solution.py:341
  230.6 0.1 reduce-scatter.7.cloned.1.call-update
  230.6 0.1 reduce-scatter.9.cloned.1.call-start
  230.7 20.5 %up_grad.4 = bf16[1024,3200]{1,0:T(8,128)(2,1)} custom-call(bf16[2048,1024]{1,0:T(8,128)(2,1)} %get-tuple-element.28.a_ref, bf16[2048,3200]{1,0:T(8,128)(2,1)} %get-tuple-element.37.b_ref.g_ref), custom_call_target="tpu_custom_call" | custom-call | flops 13421772800 | bytes 30000000 | tf_op jit(solution)/shard_map/up_grad/pallas_call | solution.py:357
  251.2 0.1 reduce-scatter.9.cloned.1.call-update
  251.2 0.1 reduce-scatter.11.cloned.1.call-start
  251.3 20.4 %up_grad.5 = bf16[1024,3200]{1,0:T(8,128)(2,1)} custom-call(bf16[2048,1024]{1,0:T(8,128)(2,1)} %get-tuple-element.28.a_ref, bf16[2048,3200]{1,0:T(8,128)(2,1)} %get-tuple-element.36.b_ref.u_ref), custom_call_target="tpu_custom_call" | custom-call | flops 13421772800 | bytes 30000000 | tf_op jit(solution)/shard_map/up_grad/pallas_call | solution.py:357
  271.7 0.1 reduce-scatter.11.cloned.1.call-update
  271.8 0.1 reduce-scatter.17.cloned.1.call-start
  271.8 2.1 reduce-scatter.7.cloned.1.call-done
  273.9 41.3 %input_grad.2.b_ref.dy_ref.dh_ref = bf16[2048,1024]{1,0:T(8,128)(2,1)} custom-call(bf16[2048,3200]{1,0:T(8,128)(2,1)} %get-tuple-element.37.b_ref.g_ref, bf16[2048,3200]{1,0:T(8,128)(2,1)} %get-tuple-element.36.b_ref.u_ref, bf16[1024,3200]{1,0:T(8,128)(2,1)} %get-tuple-element.29.wg_ref, bf16[1024,3200]{1,0:T(8,128)(2,1)} %get-tuple-element.30.wu_ref, ...), custom_call_target="tpu_custom_call" | custom-call | flops 26843545600 | bytes 50000000 | tf_op jit(solution)/shard_map/input_grad/pallas_call | solution.py:381
  315.1 0.4 reduce-scatter.9.cloned.1.call-done
  315.5 18.6 %down_grad.3 = bf16[3200,1024]{1,0:T(8,128)(2,1)} custom-call(bf16[2048,3200]{1,0:T(8,128)(2,1)} %get-tuple-element.39.a_ref, bf16[2048,1024]{1,0:T(8,128)(2,1)} %input_grad.2.b_ref.dy_ref.dh_ref), custom_call_target="tpu_custom_call" | custom-call | flops 13421772800 | bytes 30000000 | tf_op jit(solution)/shard_map/down_grad/pallas_call | solution.py:341
  334.1 0.1 reduce-scatter.17.cloned.1.call-update
  334.2 0.1 reduce-scatter.13.cloned.1.call-start
  334.3 52.5 %inner_backward.3 = (bf16[2048,3200]{1,0:T(8,128)(2,1)}, bf16[2048,3200]{1,0:T(8,128)(2,1)}) custom-call(bf16[2048,1024]{1,0:T(8,128)(2,1)} %get-tuple-element.27.a_ref, bf16[2048,1024]{1,0:T(8,128)(2,1)} %input_grad.2.b_ref.dy_ref.dh_ref, bf16[1024,3200]{1,0:T(8,128)(2,1)} %get-tuple-element.42.wg_ref, bf16[1024,3200]{1,0:T(8,128)(2,1)} %get-tuple-element.43.wu_ref, ...), custom_call_target="tpu_custom_call" | custom-call | flops 40265318400 | bytes 60000000 | tf_op jit(solution)/shard_map/inner_backward/pallas_call | solution.py:325
  386.8 0.0 reduce-scatter.11.cloned.1.call-done
  386.8 20.5 %up_grad.6 = bf16[1024,3200]{1,0:T(8,128)(2,1)} custom-call(bf16[2048,1024]{1,0:T(8,128)(2,1)} %get-tuple-element.27.a_ref, bf16[2048,3200]{1,0:T(8,128)(2,1)} %get-tuple-element.49.b_ref.g_ref), custom_call_target="tpu_custom_call" | custom-call | flops 13421772800 | bytes 30000000 | tf_op jit(solution)/shard_map/up_grad/pallas_call | solution.py:357
  407.3 0.1 reduce-scatter.13.cloned.1.call-update
  407.4 0.1 reduce-scatter.15.cloned.1.call-start
  407.4 20.3 %up_grad.7 = bf16[1024,3200]{1,0:T(8,128)(2,1)} custom-call(bf16[2048,1024]{1,0:T(8,128)(2,1)} %get-tuple-element.27.a_ref, bf16[2048,3200]{1,0:T(8,128)(2,1)} %get-tuple-element.48.b_ref.u_ref), custom_call_target="tpu_custom_call" | custom-call | flops 13421772800 | bytes 30000000 | tf_op jit(solution)/shard_map/up_grad/pallas_call | solution.py:357
  427.7 0.1 reduce-scatter.15.cloned.1.call-update
  427.8 0.0 copy-start
  427.8 0.0 copy-start.1
  427.8 41.3 %input_grad.3 = bf16[2048,1024]{1,0:T(8,128)(2,1)} custom-call(bf16[2048,3200]{1,0:T(8,128)(2,1)} %get-tuple-element.49.b_ref.g_ref, bf16[2048,3200]{1,0:T(8,128)(2,1)} %get-tuple-element.48.b_ref.u_ref, bf16[1024,3200]{1,0:T(8,128)(2,1)} %get-tuple-element.42.wg_ref, bf16[1024,3200]{1,0:T(8,128)(2,1)} %get-tuple-element.43.wu_ref, ...), custom_call_target="tpu_custom_call" | custom-call | flops 26843545600 | bytes 50000000 | tf_op jit(solution)/shard_map/input_grad/pallas_call | solution.py:381
  469.1 0.0 copy-start.2
  469.1 0.0 reduce-scatter.17.cloned.1.call-done
  469.1 0.0 copy-done
  469.1 2.5 pad_maximum_fusion.2
  471.6 0.0 reduce-scatter.13.cloned.1.call-done
  471.6 0.0 copy-done.1
  471.6 2.5 pad_maximum_fusion
  474.1 15.7 %reduce-scatter.15.cloned.1.call-done = bf16[128,3200]{1,0:T(8,128)(2,1)} async-done(((bf16[1024,3200]{1,0:T(8,128)(2,1)}), bf16[128,3200]{1,0:T(8,128)(2,1)}) %reduce-scatter.15.cloned.1.call-update) | async-done | bytes 819216 | tf_op jit(solution)/shard_map/reduce_scatter | solution.py:399
  489.8 0.0 copy-done.2
  489.8 2.5 pad_maximum_fusion.1
Async XLA Ops:
  7.2 266.7 %reduce-scatter.7.cloned.1.call-start = ((), (), s32[]{:S(2)}) async-start(), calls=%async_computation.6 | async-start | bytes 7372800 | tf_op jit(solution)/shard_map/reduce_scatter | solution.py:399
  230.6 84.9 %reduce-scatter.9.cloned.1.call-start = ((), (), s32[]{:S(2)}) async-start(), calls=%async_computation.7 | async-start | bytes 7372800 | tf_op jit(solution)/shard_map/reduce_scatter | solution.py:399
  251.2 135.6 %reduce-scatter.11.cloned.1.call-start = ((), (), s32[]{:S(2)}) async-start(), calls=%async_computation.8 | async-start | bytes 7372800 | tf_op jit(solution)/shard_map/reduce_scatter | solution.py:399
  271.8 197.3 %reduce-scatter.17.cloned.1.call-start = ((), (), s32[]{:S(2)}) async-start(), calls=%async_computation.11 | async-start | bytes 7372800 | tf_op jit(solution)/shard_map/reduce_scatter | solution.py:399
  334.2 137.4 %reduce-scatter.13.cloned.1.call-start = ((), (), s32[]{:S(2)}) async-start(), calls=%async_computation.9 | async-start | bytes 7372800 | tf_op jit(solution)/shard_map/reduce_scatter | solution.py:399
  407.4 82.4 %reduce-scatter.15.cloned.1.call-start = ((), (), s32[]{:S(2)}) async-start(), calls=%async_computation.10 | async-start | bytes 7372800 | tf_op jit(solution)/shard_map/reduce_scatter | solution.py:399
  427.8 41.3 %copy-start = (bf16[400,1024]{1,0:T(8,128)(2,1)S(1)}, bf16[400,1024]{1,0:T(8,128)(2,1)}, u32[]{:S(2)}) copy-start(bf16[400,1024]{1,0:T(8,128)(2,1)} %reduce-scatter.7.cloned.1.call-done) | copy-start | bytes 2457604
  427.8 43.9 %copy-start.1 = (bf16[128,3200]{1,0:T(8,128)(2,1)S(1)}, bf16[128,3200]{1,0:T(8,128)(2,1)}, u32[]{:S(2)}) copy-start(bf16[128,3200]{1,0:T(8,128)(2,1)} %reduce-scatter.9.cloned.1.call-done) | copy-start | bytes 2457604
  469.1 20.7 %copy-start.2 = (bf16[128,3200]{1,0:T(8,128)(2,1)S(1)}, bf16[128,3200]{1,0:T(8,128)(2,1)}, u32[]{:S(2)}) copy-start(bf16[128,3200]{1,0:T(8,128)(2,1)} %reduce-scatter.11.cloned.1.call-done) | copy-start | bytes 2457604
Sparse Core Ops, SparseCore 0:
  230.7 43.1 reduce-scatter.6
  276.2 39.2 reduce-scatter.8
  317.8 39.2 reduce-scatter.10
  359.3 39.2 reduce-scatter.16
  407.5 40.8 reduce-scatter.12
  450.5 39.2 reduce-scatter.14

commit v2 on v1

--- a/solution.py
+++ b/solution.py
@@ -230,28 +230,28 @@
     late(2)
     gate_up(3, 7)
     last(2)
-    gate_up(7, 9)
+    gate_up(7, 8)
     mid(3)
     start(5)
-    gate_up(9, full)
+    gate_up(8, 11)
+    late(3)
+    gate_up(11, full)
     done(2)
     wd_load = pltpu.make_async_copy(gathered[2], wd_v, row_sem.at[1])
     wd_load.start()
     if rest:
         act_tile(full, full % 2, rest)
-    late(3)
+    last(3)
+    mid(4)
     a_out.wait()
     wd_load.wait()
-    down(0, 2)
-    last(3)
-    down(2, 4)
-    mid(4)
-    down(4, T // mt)
+    down(0, 5)
+    late(4)
+    down(5, T // mt)
     h_out = pltpu.make_async_copy(x_v, h1_ref, row_sem.at[0])
     h_out.start()
     a1_out = pltpu.make_async_copy(a_v, a1_ref, row_sem.at[1])
     a1_out.start()
-    late(4)
     mid(5)
     last(4)
     late(5)
@@ -367,9 +367,23 @@
     D = wg.shape[0]
     mt = 256
 
-    def body(g_ref, u_ref, wg_ref, wu_ref, h_ref, dh_ref, o_ref):
-        p = rounded(dot(g_ref[...], wg_ref[...], 1, 1))
-        q = rounded(dot(u_ref[...], wu_ref[...], 1, 1))
+    def body(g_ref, u_ref, wg_ref, wu_ref, h_ref, dh_ref, o_ref, wg_v, wu_v, sem):
+        loads = [pltpu.make_async_copy(wg_ref, wg_v, sem.at[0]), pltpu.make_async_copy(wu_ref, wu_v, sem.at[1])]
+        first = pl.program_id(0) == 0
+
+        @pl.when(first)
+        def _():
+            loads[0].start()
+            loads[1].start()
+            loads[0].wait()
+
+        p = rounded(dot(g_ref[...], wg_v[...], 1, 1))
+
+        @pl.when(first)
+        def _():
+            loads[1].wait()
+
+        q = rounded(dot(u_ref[...], wu_v[...], 1, 1))
         d = rounded(p + q)
         w = h_ref[...].astype(F32)
         sc = lax.rsqrt(jnp.mean(w * w, -1, keepdims=True) + EPS)
@@ -379,7 +393,8 @@
 
     tf, td = pl.BlockSpec((mt, FF), lambda m: (m, 0)), pl.BlockSpec((mt, D), lambda m: (m, 0))
     return pl.pallas_call(
-        body, name="input_grad", grid=(T // mt,), in_specs=[tf, tf, whole((D, FF)), whole((D, FF)), td, td], out_specs=td,
+        body, name="input_grad", grid=(T // mt,), in_specs=[tf, tf, ANY, ANY, td, td], out_specs=td,
+        scratch_shapes=[pltpu.VMEM((D, FF), BF), pltpu.VMEM((D, FF), BF), pltpu.SemaphoreType.DMA((2,))],
         out_shape=jax.ShapeDtypeStruct((T, D), BF), compiler_params=params(1), cost_estimate=cost(4 * T * D * FF, 5e7),
     )(dgate, dup, wg, wu, h, dh)
 

time: 508 us -> 500 us (0.984)
  transfers between devices with their start and end apart: 6 -> 6, of which waited for: 3 -> 3; matrix products, arithmetic and copies ran while one was open for 1% -> 1% of each run, Pallas kernels for 47% -> 48%
where the time goes in v2:
time: 500 us; the launch traced here: 493 us
  Pallas kernels  454 us (91%)
  waiting for transfers between devices  16.3 us (3%)
  between operations  14.4 us (3%)
  other arithmetic  7.51 us (2%)
    pallas_call x1, Pallas kernels, forward(): pl.pallas_call(functools.partial(forward_kernel, n), name='gather_forward...  147 us
    pallas_call x2, Pallas kernels, inner_backward(): pl.pallas_call(body, name='inner_backward', grid=(pl.cdiv(FF, ft),), in_s...  105 us
    pallas_call x2, Pallas kernels, input_grad(): pl.pallas_call(body, name='input_grad', grid=(T // mt,), in_specs=[tf, tf...  83.2 us
    pallas_call x4, Pallas kernels, up_grad(): pl.pallas_call(body, name='up_grad', grid=(pl.cdiv(FF, ft),), in_specs=[w...  81.5 us
    pallas_call x2, Pallas kernels, down_grad(): pl.pallas_call(body, name='down_grad', grid=(FF // ft,), in_specs=[pl.Blo...  37.4 us
    reduce_scatter x6, waiting for transfers between devices, scattered(): return lax.psum_scatter(t, 'dp', scatter_dimension=0, tiled=True)  16 us
  transfers between devices with their start and end apart: 6, of which 3 were waited for; matrix products, arithmetic and copies ran while one was open for 1% of the time, Pallas kernels for 48%

profile of v2, /device:TPU:112, one launch (start us, length us, event | category | flops | bytes accessed | tf_op | source)
XLA Modules:
  0.0 493.1 jit_solution(16778656918425296028)
XLA Ops:
  7.2 0.1 reduce-scatter.7.cloned.1.call-start
  7.2 147.1 %gather_forward.1 = (bf16[1024,3200]{1,0:T(8,128)(2,1)}, bf16[1024,3200]{1,0:T(8,128)(2,1)}, bf16[3200,1024]{1,0:T(8,128)(2,1)}, bf16[1024,3200]{1,0:T(8,128)(2,...) custom-call(bf16[2048,1024]{1,0:T(8,128)(2,1)} %bitcast.18, ...), custom_call_target="tpu_custom_call" | custom-call | flops 40265318400 | bytes 200000000 | tf_op jit(solution)/shard_map/gather_forward/pallas_call | solution.py:277
  154.3 52.8 %inner_backward.2 = (bf16[2048,3200]{1,0:T(8,128)(2,1)}, bf16[2048,3200]{1,0:T(8,128)(2,1)}, bf16[2048,3200]{1,0:T(8,128)(2,1)}) custom-call(bf16[2048,1024]{1,0:T(8,128)(2,1)} %get-tuple-element.28.a_ref, bf16[2048,1024]{1,0:T(8,128)(2,1)} %bitcast.15, bf16[1024,3200]{1,0:T(8,128)(2,1)} %get-tuple-element.29.wg_ref, ...), custom_call_target="tpu_custom_call" | custom-call | flops 40265318400 | bytes 60000000 | tf_op jit(solution)/shard_map/inner_backward/pallas_call | solution.py:325
  207.1 18.8 %down_grad.2 = bf16[3200,1024]{1,0:T(8,128)(2,1)} custom-call(bf16[2048,3200]{1,0:T(8,128)(2,1)} %get-tuple-element.34.a_ref, bf16[2048,1024]{1,0:T(8,128)(2,1)} %bitcast.16), custom_call_target="tpu_custom_call" | custom-call | flops 13421772800 | bytes 30000000 | tf_op jit(solution)/shard_map/down_grad/pallas_call | solution.py:341
  225.9 0.1 reduce-scatter.7.cloned.1.call-update
  226.0 0.1 reduce-scatter.9.cloned.1.call-start
  226.0 20.3 %up_grad.4 = bf16[1024,3200]{1,0:T(8,128)(2,1)} custom-call(bf16[2048,1024]{1,0:T(8,128)(2,1)} %get-tuple-element.28.a_ref, bf16[2048,3200]{1,0:T(8,128)(2,1)} %get-tuple-element.37.b_ref.g_ref), custom_call_target="tpu_custom_call" | custom-call | flops 13421772800 | bytes 30000000 | tf_op jit(solution)/shard_map/up_grad/pallas_call | solution.py:357
  246.3 0.1 reduce-scatter.9.cloned.1.call-update
  246.4 0.1 reduce-scatter.11.cloned.1.call-start
  246.5 20.4 %up_grad.5 = bf16[1024,3200]{1,0:T(8,128)(2,1)} custom-call(bf16[2048,1024]{1,0:T(8,128)(2,1)} %get-tuple-element.28.a_ref, bf16[2048,3200]{1,0:T(8,128)(2,1)} %get-tuple-element.36.b_ref.u_ref), custom_call_target="tpu_custom_call" | custom-call | flops 13421772800 | bytes 30000000 | tf_op jit(solution)/shard_map/up_grad/pallas_call | solution.py:357
  266.9 0.1 reduce-scatter.11.cloned.1.call-update
  266.9 0.1 reduce-scatter.17.cloned.1.call-start
  267.0 0.7 reduce-scatter.7.cloned.1.call-done
  267.7 41.4 %input_grad.2.b_ref.dy_ref.dh_ref = bf16[2048,1024]{1,0:T(8,128)(2,1)} custom-call(bf16[2048,3200]{1,0:T(8,128)(2,1)} %get-tuple-element.37.b_ref.g_ref, bf16[2048,3200]{1,0:T(8,128)(2,1)} %get-tuple-element.36.b_ref.u_ref, bf16[1024,3200]{1,0:T(8,128)(2,1)} %get-tuple-element.29.wg_ref, bf16[1024,3200]{1,0:T(8,128)(2,1)} %get-tuple-element.30.wu_ref, ...), custom_call_target="tpu_custom_call" | custom-call | flops 26843545600 | bytes 50000000 | tf_op jit(solution)/shard_map/input_grad/pallas_call | solution.py:395
  309.1 0.2 reduce-scatter.9.cloned.1.call-done
  309.3 18.6 %down_grad.3 = bf16[3200,1024]{1,0:T(8,128)(2,1)} custom-call(bf16[2048,3200]{1,0:T(8,128)(2,1)} %get-tuple-element.39.a_ref, bf16[2048,1024]{1,0:T(8,128)(2,1)} %input_grad.2.b_ref.dy_ref.dh_ref), custom_call_target="tpu_custom_call" | custom-call | flops 13421772800 | bytes 30000000 | tf_op jit(solution)/shard_map/down_grad/pallas_call | solution.py:341
  327.9 0.1 reduce-scatter.17.cloned.1.call-update
  328.0 0.1 reduce-scatter.13.cloned.1.call-start
  328.1 52.5 %inner_backward.3 = (bf16[2048,3200]{1,0:T(8,128)(2,1)}, bf16[2048,3200]{1,0:T(8,128)(2,1)}) custom-call(bf16[2048,1024]{1,0:T(8,128)(2,1)} %get-tuple-element.27.a_ref, bf16[2048,1024]{1,0:T(8,128)(2,1)} %input_grad.2.b_ref.dy_ref.dh_ref, bf16[1024,3200]{1,0:T(8,128)(2,1)} %get-tuple-element.42.wg_ref, bf16[1024,3200]{1,0:T(8,128)(2,1)} %get-tuple-element.43.wu_ref, ...), custom_call_target="tpu_custom_call" | custom-call | flops 40265318400 | bytes 60000000 | tf_op jit(solution)/shard_map/inner_backward/pallas_call | solution.py:325
  380.6 0.0 reduce-scatter.11.cloned.1.call-done
  380.6 20.5 %up_grad.6 = bf16[1024,3200]{1,0:T(8,128)(2,1)} custom-call(bf16[2048,1024]{1,0:T(8,128)(2,1)} %get-tuple-element.27.a_ref, bf16[2048,3200]{1,0:T(8,128)(2,1)} %get-tuple-element.49.b_ref.g_ref), custom_call_target="tpu_custom_call" | custom-call | flops 13421772800 | bytes 30000000 | tf_op jit(solution)/shard_map/up_grad/pallas_call | solution.py:357
  401.1 0.1 reduce-scatter.13.cloned.1.call-update
  401.2 0.1 reduce-scatter.15.cloned.1.call-start
  401.2 20.3 %up_grad.7 = bf16[1024,3200]{1,0:T(8,128)(2,1)} custom-call(bf16[2048,1024]{1,0:T(8,128)(2,1)} %get-tuple-element.27.a_ref, bf16[2048,3200]{1,0:T(8,128)(2,1)} %get-tuple-element.48.b_ref.u_ref), custom_call_target="tpu_custom_call" | custom-call | flops 13421772800 | bytes 30000000 | tf_op jit(solution)/shard_map/up_grad/pallas_call | solution.py:357
  421.5 0.1 reduce-scatter.15.cloned.1.call-update
  421.6 0.0 copy-start
  421.6 0.0 copy-start.1
  421.6 41.8 %input_grad.3 = bf16[2048,1024]{1,0:T(8,128)(2,1)} custom-call(bf16[2048,3200]{1,0:T(8,128)(2,1)} %get-tuple-element.49.b_ref.g_ref, bf16[2048,3200]{1,0:T(8,128)(2,1)} %get-tuple-element.48.b_ref.u_ref, bf16[1024,3200]{1,0:T(8,128)(2,1)} %get-tuple-element.42.wg_ref, bf16[1024,3200]{1,0:T(8,128)(2,1)} %get-tuple-element.43.wu_ref, ...), custom_call_target="tpu_custom_call" | custom-call | flops 26843545600 | bytes 50000000 | tf_op jit(solution)/shard_map/input_grad/pallas_call | solution.py:395
  463.4 0.0 copy-start.2
  463.4 0.0 reduce-scatter.17.cloned.1.call-done
  463.4 0.0 copy-done
  463.4 2.5 pad_maximum_fusion.2
  466.0 0.0 reduce-scatter.13.cloned.1.call-done
  466.0 0.0 copy-done.1
  466.0 2.5 pad_maximum_fusion
  468.4 15.1 %reduce-scatter.15.cloned.1.call-done = bf16[128,3200]{1,0:T(8,128)(2,1)} async-done(((bf16[1024,3200]{1,0:T(8,128)(2,1)}), bf16[128,3200]{1,0:T(8,128)(2,1)}) %reduce-scatter.15.cloned.1.call-update) | async-done | bytes 819216 | tf_op jit(solution)/shard_map/reduce_scatter | solution.py:414
  483.6 0.0 copy-done.2
  483.6 2.5 pad_maximum_fusion.1
Async XLA Ops:
  7.2 260.5 %reduce-scatter.7.cloned.1.call-start = ((), (), s32[]{:S(2)}) async-start(), calls=%async_computation.6 | async-start | bytes 7372800 | tf_op jit(solution)/shard_map/reduce_scatter | solution.py:414
  226.0 83.3 %reduce-scatter.9.cloned.1.call-start = ((), (), s32[]{:S(2)}) async-start(), calls=%async_computation.7 | async-start | bytes 7372800 | tf_op jit(solution)/shard_map/reduce_scatter | solution.py:414
  246.4 134.2 %reduce-scatter.11.cloned.1.call-start = ((), (), s32[]{:S(2)}) async-start(), calls=%async_computation.8 | async-start | bytes 7372800 | tf_op jit(solution)/shard_map/reduce_scatter | solution.py:414
  266.9 196.5 %reduce-scatter.17.cloned.1.call-start = ((), (), s32[]{:S(2)}) async-start(), calls=%async_computation.11 | async-start | bytes 7372800 | tf_op jit(solution)/shard_map/reduce_scatter | solution.py:414
  328.0 138.0 %reduce-scatter.13.cloned.1.call-start = ((), (), s32[]{:S(2)}) async-start(), calls=%async_computation.9 | async-start | bytes 7372800 | tf_op jit(solution)/shard_map/reduce_scatter | solution.py:414
  401.2 82.4 %reduce-scatter.15.cloned.1.call-start = ((), (), s32[]{:S(2)}) async-start(), calls=%async_computation.10 | async-start | bytes 7372800 | tf_op jit(solution)/shard_map/reduce_scatter | solution.py:414
  421.6 41.8 %copy-start = (bf16[400,1024]{1,0:T(8,128)(2,1)S(1)}, bf16[400,1024]{1,0:T(8,128)(2,1)}, u32[]{:S(2)}) copy-start(bf16[400,1024]{1,0:T(8,128)(2,1)} %reduce-scatter.7.cloned.1.call-done) | copy-start | bytes 2457604
  421.6 44.4 %copy-start.1 = (bf16[128,3200]{1,0:T(8,128)(2,1)S(1)}, bf16[128,3200]{1,0:T(8,128)(2,1)}, u32[]{:S(2)}) copy-start(bf16[128,3200]{1,0:T(8,128)(2,1)} %reduce-scatter.9.cloned.1.call-done) | copy-start | bytes 2457604
  463.4 20.2 %copy-start.2 = (bf16[128,3200]{1,0:T(8,128)(2,1)S(1)}, bf16[128,3200]{1,0:T(8,128)(2,1)}, u32[]{:S(2)}) copy-start(bf16[128,3200]{1,0:T(8,128)(2,1)} %reduce-scatter.11.cloned.1.call-done) | copy-start | bytes 2457604
Sparse Core Ops, SparseCore 0:
  226.1 41.5 reduce-scatter.6
  270.0 39.2 reduce-scatter.8
  311.6 39.2 reduce-scatter.10
  353.1 39.2 reduce-scatter.16
  401.3 40.8 reduce-scatter.12
  444.3 39.2 reduce-scatter.14
